TPU v7x, 32 devices: a whole 2x2x4 slice. The times are simulated.
32 devices in a mesh: node: 4 (over y, x), intra: 8 (over z, core).
Axes of the slice: x: 2, y: 2, z: 4, core: 2. Of those that a mesh axis runs over, the one named last changes fastest.
Arguments:
- gradients: bfloat16 [4, 8, 3072, 512], P('node', 'intra'), as said below
- sign_table: int32 [64, 512], replicated, may hold values from -1 to 1, as said below
- loss_scale: float32 [1], replicated, may hold values from 256 to 65536
- step_count: int32 [1], replicated, may hold values from 1 to 8
- weights: float32 [3072, 512], P('intra', 'node'), may hold values from -6 to 6
- first_moment: float32 [3072, 512], P('intra', 'node'), may hold values from -3 to 3
- second_moment: float32 [3072, 512], P('intra', 'node'), may hold values from 0.01 to 0.1
Outputs:
- new_weights: float32 [3072, 512], P('intra', 'node')
- new_first: float32 [3072, 512], P('intra', 'node')
- new_second: float32 [3072, 512], P('intra', 'node')
Inputs may be any that keep to these rules, and one draw needn't show every extreme that they name: `gradients`: each replica's gradient is multiplied by loss_scale. `sign_table`: every entry is -1 or 1.
All inputs are finite; a program needn't handle non-finite values.
Results may differ from a plain program's by a relative error of at most 0.0003.
Values sent between devices are 32-bit elements; how exact they have to be, the bound alone decides.
A program may use at most 128 MiB of HBM per device.

v0:
```python
import contextlib
import functools
import math

import jax
import jax.numpy as jnp
from jax import lax
from jax.experimental import pallas as pl
from jax.experimental.pallas import tpu as pltpu
from jax.sharding import PartitionSpec as P

BLOCK = 128
WIDE = 2 * BLOCK
SIGN_ROWS = 64
CORES = 2
SLOTS = 8
SUBS = 2
CHUNKS = 3
ROOT = 1.0 / math.sqrt(BLOCK)
MESH = pl.DeviceIdType.MESH


def scope(name):
    return contextlib.nullcontext()


def parity_sign(rows, columns):
    common = lax.broadcasted_iota(jnp.int32, (rows, columns), 0) & lax.broadcasted_iota(
        jnp.int32, (rows, columns), 1
    ) & (BLOCK - 1)
    parity = common
    for bit_index in range(1, BLOCK.bit_length() - 1):
        parity = parity ^ (common >> bit_index)
    return (1 - 2 * (parity & 1)).astype(jnp.float32)


def paired_table():
    row = lax.broadcasted_iota(jnp.int32, (WIDE, WIDE), 0) // BLOCK
    column = lax.broadcasted_iota(jnp.int32, (WIDE, WIDE), 1) // BLOCK
    return jnp.where(row == column, parity_sign(WIDE, WIDE), 0.0).astype(jnp.bfloat16)


def plan_rows(owned):
    z_rows = owned * 5 // 24 // 16 * 16
    return z_rows, (owned - z_rows) // 2


def reduce_kernel(
    n_node, n_intra, grad_ref, sign_ref, scale_ref, step_ref, weight_ref, first_ref, second_ref,
    sum_ref, aux_ref, sign_out, weight_out, first_out, second_out,
    stage, sign_tab, sign_bf, table_bf, lev, levz, pair, pairz, raw, zraw, first, second, third, agg,
    zin, zfirst, zsecond, peaks,
    load_sem, side_sem, pair_send, pair_recv, pairz_send, pairz_recv, raw_send, raw_recv,
    zraw_send, zraw_recv, first_send, first_recv, second_send, second_recv, third_send, third_recv,
    agg_send, agg_recv, zin_send, zin_recv, zfirst_send, zfirst_recv, zsecond_send, zsecond_recv,
    peak_send, peak_recv,
):
    n_z = n_intra // CORES
    last = n_z - 1
    n_dev = n_node * n_intra
    owned = sum_ref.shape[0]
    z_rows, half = plan_rows(owned)
    zh = z_rows // 2
    cut = (half // SUBS + 7) // 8 * 8
    spans = ((0, cut), (cut, half - cut))
    raw_rows = half * 7 // 10 // 8 * 8
    raw_spans = ((0, raw_rows), (raw_rows, half - raw_rows))
    node, intra = lax.axis_index("node"), lax.axis_index("intra")
    z, core = intra // CORES, intra % CORES
    hi, lo = node // 2, node % 2
    me = node * n_intra + intra
    end = (z == 0) | (z == last)
    near = (z == 1) | (z == last - 1)
    inward = jnp.where(z == 0, 1, last - 1)

    def at(node_index, z_index, core_index):
        return (node_index, z_index * CORES + core_index)

    def flat(index):
        return (index // n_intra, index % n_intra)

    def send(src, dst, send_sem, recv_sem, device):
        return pltpu.make_async_remote_copy(
            src_ref=src, dst_ref=dst, send_sem=send_sem, recv_sem=recv_sem,
            device_id=device, device_id_type=MESH,
        )

    def piece(k):
        lower = jnp.where(k < last - z, last - k, k - (last - z))
        upper = jnp.where(k < z, k, last - (k - z))
        return jnp.where(z < n_z // 2, lower, upper)

    def block_at(q):
        return piece(q // CORES) * CORES + jnp.where(q % CORES == 0, core, 1 - core)

    def load(q):
        slot = lax.rem(q, SLOTS)
        return pltpu.make_async_copy(
            grad_ref.at[pl.ds(block_at(q) * owned, owned)], stage.at[slot], load_sem.at[slot]
        )

    sides = [
        pltpu.make_async_copy(src, dst, side_sem.at[n])
        for n, (src, dst) in enumerate((
            (sign_ref, sign_tab), (weight_ref, weight_out), (first_ref, first_out), (second_ref, second_out),
        ))
    ]
    sides[0].start()
    for q in range(min(SLOTS, n_intra)):
        load(q).start()
    for copy in sides[1:]:
        copy.start()

    barrier = pltpu.get_barrier_semaphore()

    def greet(step, carry):
        pl.semaphore_signal(
            barrier, inc=1, device_id=flat(lax.rem(me + step, n_dev)), device_id_type=MESH
        )
        return carry

    lax.fori_loop(1, n_dev, greet, 0)
    table_bf[...] = paired_table()
    with scope("Asign"):
        sides[0].wait()
        sign_bf[...] = sign_tab[...].astype(jnp.float32).astype(jnp.bfloat16)

    def rotate(q, most):
        load(q).wait()
        i = block_at(q)
        block = stage[lax.rem(q, SLOTS)]
        for w in range(n_node // 2):
            cols = slice(w * WIDE, (w + 1) * WIDE)
            part = block[:, cols].reshape(owned // SIGN_ROWS, SIGN_ROWS, WIDE)
            signed = (part * sign_bf[:, cols][None]).reshape(owned, WIDE)
            both = jnp.dot(signed, table_bf[...], preferred_element_type=jnp.float32)
            for v in range(2):
                spun = both[:, v * BLOCK : (v + 1) * BLOCK]
                for h in range(2):
                    lev[i, w, v, h] = spun[h * half : (h + 1) * half]
                levz[i, w, v] = spun[2 * half :]
                most = jnp.maximum(
                    most, jnp.max(jnp.abs(spun).reshape(owned // 8, 8, BLOCK), axis=0)
                )

        @pl.when(q + SLOTS < n_intra)
        def _():
            load(q + SLOTS).start()

        return most

    lo_peer = hi * 2 + 1 - lo
    hi_peer = (1 - hi) * 2 + lo

    def pair_copy(p):
        other = p * CORES + 1 - core
        return send(
            lev.at[other], pair.at[p], pair_send.at[p], pair_recv.at[p], at(node, z, 1 - core)
        )

    def pairz_copy(p):
        other = p * CORES + 1 - core
        return send(
            levz.at[other], pairz.at[p], pairz_send.at[p], pairz_recv.at[p], at(node, z, 1 - core)
        )

    def raw_copies(flip):
        target = core if flip == 0 else 1 - core
        i, r = piece(0) * CORES + target, pl.ds(0, raw_rows)
        return [
            send(
                src, raw.at[flip, h], raw_send.at[flip, h], raw_recv.at[flip, h],
                at(peer, z, target),
            )
            for h, src, peer in (
                (0, lev.at[i, :, 1 - lo, 0, r], lo_peer),
                (1, lev.at[i, 1 - hi, :, 1, r], hi_peer),
            )
        ]

    def zraw_copy(flip):
        target = core if flip == 0 else 1 - core
        return send(
            levz.at[piece(0) * CORES + target, :, :, z_part(0)], zraw.at[flip], zraw_send.at[flip], zraw_recv.at[flip],
            at(node, inward, target),
        )

    def rows_of(s, lead=False):
        return pl.ds(*(raw_spans if lead else spans)[s])

    def first_copies(p, s, lead=False):
        i, r = p * CORES + core, rows_of(s, lead)
        return [
            send(
                src, first.at[p, h, :, r], first_send.at[h, p * SUBS + s],
                first_recv.at[h, p * SUBS + s], at(peer, z, core),
            )
            for h, src, peer in (
                (0, lev.at[i, :, 1 - lo, 0, r], lo_peer),
                (1, lev.at[i, 1 - hi, :, 1, r], hi_peer),
            )
        ]

    def second_copies(p, s, lead=False):
        i, r = p * CORES + core, rows_of(s, lead)
        return [
            send(
                src, second.at[p, h, r], second_send.at[h, p * SUBS + s],
                second_recv.at[h, p * SUBS + s], at(peer, z, core),
            )
            for h, src, peer in (
                (0, lev.at[i, 1 - hi, lo, 0, r], hi_peer),
                (1, lev.at[i, hi, 1 - lo, 1, r], lo_peer),
            )
        ]

    def third_copy(p, slot, s):
        r = rows_of(s)
        return send(
            lev.at[p * CORES + core, hi, lo, :, r], third.at[slot, :, r],
            third_send.at[p * SUBS + s], third_recv.at[slot * SUBS + s], at(node, p, core),
        )

    def agg_copy(s):
        r = rows_of(s)
        return send(
            lev.at[piece(0) * CORES + core, hi, lo, :, r], agg.at[:, r], agg_send.at[s], agg_recv.at[s],
            at(node, inward, core),
        )

    def z_part(h):
        return pl.ds(h * zh, zh)

    def z_copy(p, h):
        onward = jnp.where(p > z, z + 1, z - 1)
        slot = jnp.where((p < z) & (p == onward), n_z, p)
        return send(
            levz.at[p * CORES + core, :, :, z_part(h)], zin.at[slot, :, :, z_part(h)],
            zin_send.at[p * 2 + h], zin_recv.at[slot * 2 + h], at(node, onward, core),
        )

    def z_arrived(slot, h):
        send(
            levz.at[core, :, :, z_part(h)], zin.at[slot, :, :, z_part(h)],
            zin_send.at[0], zin_recv.at[slot * 2 + h], at(node, inward, core),
        ).wait_recv()

    def z_first_copies():
        return [
            send(src, zfirst.at[h], zfirst_send.at[h], zfirst_recv.at[h], at(peer, z, core))
            for h, src, peer in (
                (0, levz.at[intra, :, 1 - lo, z_part(0)], lo_peer),
                (1, levz.at[intra, 1 - hi, :, z_part(1)], hi_peer),
            )
        ]

    def z_second_copies():
        return [
            send(src, zsecond.at[h], zsecond_send.at[h], zsecond_recv.at[h], at(peer, z, core))
            for h, src, peer in (
                (0, levz.at[intra, 1 - hi, lo, z_part(0)], hi_peer),
                (1, levz.at[intra, hi, 1 - lo, z_part(1)], lo_peer),
            )
        ]

    def peak_copy(target, slot):
        return send(
            peaks.at[slot], peaks.at[slot], peak_send.at[target], peak_recv.at[slot], flat(target)
        )

    with scope("A_rotate"):
        most = lax.fori_loop(0, n_intra, rotate, jnp.zeros((8, BLOCK), jnp.float32))
        peaks[me] = jnp.max(most, axis=0, keepdims=True)
    with scope("B_barrier"):
        pl.semaphore_wait(barrier, n_dev - 1)

    def tell(step, carry):
        peak_copy(lax.rem(me + step, n_dev), me).start()
        return carry

    with scope("C_issue"):
        lax.fori_loop(1, n_dev, tell, 0)
        for flip in range(2):
            for copy in raw_copies(flip):
                copy.start()

        @pl.when(end)
        def _():
            for flip in range(2):
                zraw_copy(flip).start()

        def share(k, carry):
            pair_copy(piece(k)).start()
            pairz_copy(piece(k)).start()
            return carry

        lax.fori_loop(0, n_z, share, 0)

    with scope("D_sides"):
        for copy in sides[1:]:
            copy.wait()
        ones = jnp.ones((1, BLOCK), jnp.float32)
        steps = ones * step_ref[0].astype(jnp.float32)
        aux_ref[0:1] = 1.0 / (1.0 - jnp.exp(steps * math.log(0.9)))
        aux_ref[1:2] = 1.0 / (1.0 - jnp.exp(steps * math.log(0.95)))

    def hear(step, carry):
        other = lax.rem(me + step, n_dev)
        peak_copy(other, other).wait_recv()
        return carry

    with scope("E_peaks"):
        lax.fori_loop(1, n_dev, hear, 0)
        tops = jnp.max(peaks[...], axis=0)
        top_value = jnp.max(tops, axis=1, keepdims=True) * ROOT
        level_scale = 127.0 / top_value
        factor = (ones * top_value) / (ones * (127.0 * float(n_dev) * scale_ref[0]))
        column = pl.multiple_of(node * BLOCK, BLOCK)
        sign_out[...] = sign_tab[:, pl.ds(column, BLOCK)].astype(jnp.float32) * (factor * ROOT)

    def level(value):
        return jnp.floor((value * ROOT) * level_scale + 0.5)

    def level_piece(k, s, lead=False):
        p = piece(k)
        i, r = p * CORES + core, rows_of(s, lead)
        if lead or (s == 0):
            pair_copy(p).wait_recv()
        for j in range(n_node):
            for h in range(2):
                spot = (j // 2, j % 2, h, r)
                lev[(i,) + spot] = level(lev[(i,) + spot]) + level(pair[(p,) + spot])
        for copy in first_copies(p, s, lead):
            copy.start()

    def first_sum(k, s, lead=False):
        p = piece(k)
        i, r = p * CORES + core, rows_of(s, lead)
        for copy in first_copies(p, s, lead):
            copy.wait_recv()
        for j in range(2):
            lev[i, j, lo, 0, r] = lev[i, j, lo, 0, r] + first[p, 0, j, r]
            lev[i, hi, j, 1, r] = lev[i, hi, j, 1, r] + first[p, 1, j, r]
        for copy in second_copies(p, s, lead):
            copy.start()

    def second_sum(k, s, lead=False):
        p = piece(k)
        i, r = p * CORES + core, rows_of(s, lead)
        for copy in second_copies(p, s, lead):
            copy.wait_recv()
        for h in range(2):
            lev[i, hi, lo, h, r] = lev[i, hi, lo, h, r] + second[p, h, r]

    def raw_piece():
        p = piece(0)
        i, r = p * CORES + core, rows_of(0, True)
        for flip in range(2):
            for copy in raw_copies(flip):
                copy.wait_recv()

        def kept(h, j, spot):
            lev[(i,) + spot] = (
                level(lev[(i,) + spot]) + level(pair[(p,) + spot])
                + level(raw[0, h, j]) + level(raw[1, h, j])
            )

        for j in range(2):
            kept(0, j, (j, lo, 0, r))
            kept(1, j, (hi, j, 1, r))
        for copy in second_copies(p, 0, True):
            copy.start()

    def z_level(p, h, wait):
        i, r = p * CORES + core, z_part(h)
        if wait:
            pairz_copy(p).wait_recv()
        for j in range(n_node):
            spot = (j // 2, j % 2, r)
            levz[(i,) + spot] = level(levz[(i,) + spot]) + level(pairz[(p,) + spot])

    def z_add(p, slot, h):
        i, r = p * CORES + core, z_part(h)
        z_arrived(slot, h)
        for j in range(n_node):
            spot = (j // 2, j % 2, r)
            levz[(i,) + spot] = levz[(i,) + spot] + zin[(slot,) + spot]

    def z_pass(k, h):
        p = piece(k)
        z_level(p, h, h == 0)
        z_add(p, p, h)
        z_copy(p, h).start()

    def z_inner(k, h):
        @pl.when(jnp.logical_not(end))
        def _():
            z_pass(k, h)

    def z_lead():
        @pl.when(end)
        def _():
            z_level(piece(0), 1, True)
            z_copy(piece(0), 1).start()

        @pl.when(near)
        def _():
            p = piece(0)
            i, r = p * CORES + core, z_part(0)
            z_level(p, 0, True)
            for flip in range(2):
                zraw_copy(flip).wait_recv()
            for j in range(n_node):
                spot = (j // 2, j % 2)
                levz[(i,) + spot + (r,)] = (
                    levz[(i,) + spot + (r,)]
                    + level(zraw[(0,) + spot]) + level(zraw[(1,) + spot])
                )
            z_copy(p, 0).start()

        @pl.when(jnp.logical_not(end | near))
        def _():
            z_pass(0, 0)

    def z_ahead(k):
        @pl.when(end & (k < last))
        def _():
            p = piece(k)
            for h in range(2):
                z_level(p, h, h == 0)
                z_copy(p, h).start()

    with scope("F0"):
        level_piece(0, 1, True)
        z_lead()
        level_piece(1, 0)
        z_ahead(1)
        raw_piece()
    with scope("F1"):
        z_inner(0, 1)
        level_piece(1, 1)
        z_ahead(2)
        first_sum(0, 1, True)
        second_sum(0, 0, True)
        z_inner(1, 0)
        first_sum(1, 0)
        second_sum(0, 1, True)

        @pl.when(end)
        def _():
            for s in range(SUBS):
                agg_copy(s).start()

        @pl.when(jnp.logical_not(end | near))
        def _():
            for s in range(SUBS):
                third_copy(piece(0), z, s).start()

    def z_finish():
        for h in range(2):
            z_level(z, h, h == 0)

            @pl.when(z > 0)
            def _():
                z_add(z, z, h)

            @pl.when(z < last)
            def _():
                z_add(z, n_z, h)

        for copy in z_first_copies():
            copy.start()

    def pipeline(k, carry):
        for s in range(SUBS):
            with scope("G%d" % s):
                level_piece(k, s)
                z_ahead(1 + (k - 1) * SUBS + s)
                if s == 0:
                    first_sum(k - 1, 1)

                    @pl.when(k < last)
                    def _():
                        z_inner(k - 1, 1)

                    @pl.when((k == last) & near)
                    def _():
                        p = piece(0)
                        i = p * CORES + core
                        for part in range(SUBS):
                            r = rows_of(part)
                            agg_copy(part).wait_recv()
                            for h in range(2):
                                lev[i, hi, lo, h, r] = lev[i, hi, lo, h, r] + agg[h, r]
                            third_copy(p, z, part).start()
                else:
                    first_sum(k, 0)

                    @pl.when(k < last)
                    def _():
                        z_inner(k, 0)

                    @pl.when(k == last - 1)
                    def _():
                        z_inner(k, 1)

                with scope("Gs"):
                    second_sum(k - 1, s)
                third_copy(piece(k - 1), z, s).start()
        return carry

    lax.fori_loop(2, n_z, pipeline, 0)
    with scope("H_zfinal"):
        z_finish()
    with scope("I_tail"):
        first_sum(last, 1)
        second_sum(last, 0)
    with scope("J_ztail"):
        for copy in z_first_copies():
            copy.wait_recv()
        for j in range(2):
            levz[intra, j, lo, z_part(0)] = levz[intra, j, lo, z_part(0)] + zfirst[0, j]
            levz[intra, hi, j, z_part(1)] = levz[intra, hi, j, z_part(1)] + zfirst[1, j]
        for copy in z_second_copies():
            copy.start()
    with scope("K_last"):
        second_sum(last, 1)

    def from_plane(step, carry):
        other = lax.rem(z + step, n_z)

        @pl.when(jnp.abs(other - z) != last)
        def _():
            for s in range(SUBS):
                r = rows_of(s)
                third_copy(other, other, s).wait_recv()
                for h in range(2):
                    lev[intra, hi, lo, h, r] = lev[intra, hi, lo, h, r] + third[other, h, r]

        return carry

    with scope("L_third"):
        lax.fori_loop(1, n_z, from_plane, 0)
        for h in range(2):
            sum_ref[h * half : (h + 1) * half] = lev[intra, hi, lo, h]
    with scope("M_zlast"):
        for copy in z_second_copies():
            copy.wait_recv()
        for h in range(2):
            sum_ref[2 * half + h * zh : 2 * half + (h + 1) * zh] = (
                levz[intra, hi, lo, z_part(h)] + zsecond[h]
            )

    def told(step, carry):
        peak_copy(lax.rem(me + step, n_dev), me).wait_send()
        return carry

    def finish(k, carry):
        p = piece(k)
        pair_copy(p).wait_send()
        pairz_copy(p).wait_send()

        @pl.when(k > 0)
        def _():
            for s in range(SUBS):
                for copy in first_copies(p, s) + second_copies(p, s):
                    copy.wait_send()

        @pl.when(k < last)
        def _():
            z_copy(p, 1).wait_send()

        @pl.when((k < last) & jnp.logical_not(end & (k == 0)))
        def _():
            z_copy(p, 0).wait_send()
            for s in range(SUBS):
                third_copy(p, z, s).wait_send()

        return carry

    with scope("N_finish"):
        lax.fori_loop(1, n_dev, told, 0)
        for flip in range(2):
            for copy in raw_copies(flip):
                copy.wait_send()
        p = piece(0)
        for copy in first_copies(p, 1, True) + second_copies(p, 0, True) + second_copies(p, 1, True):
            copy.wait_send()

        @pl.when(end)
        def _():
            for flip in range(2):
                zraw_copy(flip).wait_send()
            for s in range(SUBS):
                agg_copy(s).wait_send()

        lax.fori_loop(0, n_z, finish, 0)
        for copy in z_first_copies() + z_second_copies():
            copy.wait_send()


def adam_kernel(
    sum_ref, aux_ref, sign_ref, weight_ref, first_ref, second_ref,
    new_weight_ref, new_first_ref, new_second_ref, weight_buf, first_buf, second_buf, sems,
):
    owned = sum_ref.shape[0]
    table = parity_sign(WIDE, BLOCK)
    upper = lax.broadcasted_iota(jnp.int32, (WIDE, BLOCK), 0) < BLOCK
    table = jnp.where(upper, table * 64.0, table).astype(jnp.bfloat16)
    signs = sign_ref[...]
    first_unbias, second_unbias = aux_ref[0:1], aux_ref[1:2]
    rows = owned // CHUNKS
    copies = []
    for c in range(CHUNKS):
        r = slice(c * rows, (c + 1) * rows)
        summed = sum_ref[r]
        high = jnp.floor(summed * (1.0 / 64.0))
        low = summed - high * 64.0
        both = jnp.concatenate([high, low], axis=1).astype(jnp.bfloat16)
        back = jnp.dot(both, table, preferred_element_type=jnp.float32)
        grad = (back.reshape(rows // SIGN_ROWS, SIGN_ROWS, BLOCK) * signs[None]).reshape(rows, BLOCK)
        new_first = 0.9 * first_ref[r] + 0.1 * grad
        new_second = 0.95 * second_ref[r] + 0.05 * grad * grad
        first_buf[r] = new_first
        second_buf[r] = new_second
        weights = weight_ref[r]
        update = (new_first * first_unbias) / (jnp.sqrt(new_second * second_unbias) + 1e-08)
        weight_buf[r] = weights - 0.2 * (update + 0.1 * weights)
        for n, (src, dst) in enumerate((
            (first_buf, new_first_ref), (second_buf, new_second_ref), (weight_buf, new_weight_ref),
        )):
            copy = pltpu.make_async_copy(src.at[r], dst.at[r], sems.at[n, c])
            copy.start()
            copies.append(copy)
    for copy in copies:
        copy.wait()


def shards(gradients, sign_table, loss_scale, step_count, weights, first_moment, second_moment):
    n_node, n_intra = lax.axis_size("node"), lax.axis_size("intra")
    n_z = n_intra // CORES
    n_dev = n_node * n_intra
    local = gradients.reshape(gradients.shape[2:])
    rows, columns = local.shape
    owned = weights.shape[0]
    z_rows, half = plan_rows(owned)
    zh = z_rows // 2
    n_hi = n_node // 2
    anywhere = pl.BlockSpec(memory_space=pl.ANY)
    smem = pl.BlockSpec(memory_space=pltpu.SMEM)
    hbm = functools.partial(pltpu.with_memory_space_constraint, memory_space=pltpu.HBM)
    vmem = pl.BlockSpec(memory_space=pltpu.VMEM)
    dma = pltpu.SemaphoreType.DMA
    f32 = jnp.float32
    slots = min(SLOTS, n_intra)
    buffers = [
        ((slots, owned, columns), jnp.bfloat16),
        ((SIGN_ROWS, columns), jnp.int32),
        ((SIGN_ROWS, columns), jnp.bfloat16),
        ((WIDE, WIDE), jnp.bfloat16),
    ]
    large = [
        ((n_intra, n_hi, 2, 2, half, BLOCK), f32),
        ((n_intra, n_hi, 2, z_rows, BLOCK), f32),
        ((n_z, n_hi, 2, 2, half, BLOCK), f32),
        ((n_z, n_hi, 2, z_rows, BLOCK), f32),
        ((2, 2, 2, half * 7 // 10 // 8 * 8, BLOCK), f32),
        ((2, n_hi, 2, zh, BLOCK), f32),
        ((n_z, 2, 2, half, BLOCK), f32),
        ((n_z, 2, half, BLOCK), f32),
        ((n_z, 2, half, BLOCK), f32),
        ((2, half, BLOCK), f32),
        ((n_z + 1, n_hi, 2, z_rows, BLOCK), f32),
        ((2, 2, zh, BLOCK), f32),
        ((2, zh, BLOCK), f32),
        ((n_dev, 1, BLOCK), f32),
    ]
    held = sum(math.prod(shape) * jnp.dtype(kind).itemsize for shape, kind in buffers + large)
    shape = (owned, BLOCK)
    outs = pl.pallas_call(
        functools.partial(reduce_kernel, n_node, n_intra),
        out_shape=(
            pltpu.VMEM(shape, f32), pltpu.VMEM((8, BLOCK), f32), pltpu.VMEM((SIGN_ROWS, BLOCK), f32),
            pltpu.VMEM(shape, f32), pltpu.VMEM(shape, f32), pltpu.VMEM(shape, f32),
        ),
        in_specs=[anywhere] * 2 + [smem] * 2 + [anywhere] * 3,
        out_specs=(vmem,) * 6,
        scratch_shapes=[pltpu.VMEM(*b) for b in buffers]
        + [pltpu.VMEM(*b) for b in large]
        + [
            dma((slots,)), dma((4,)),
            dma((n_z,)), dma((n_z,)), dma((n_z,)), dma((n_z,)),
            dma((2, 2)), dma((2, 2)), dma((2,)), dma((2,)),
            dma((2, n_z * SUBS)), dma((2, n_z * SUBS)),
            dma((2, n_z * SUBS)), dma((2, n_z * SUBS)),
            dma((n_z * SUBS,)), dma((n_z * SUBS,)),
            dma((SUBS,)), dma((SUBS,)),
            dma((n_z * 2,)), dma((n_z * 2 + 2,)),
            dma((2,)), dma((2,)), dma((2,)), dma((2,)),
            dma((n_dev,)), dma((n_dev,)),
        ],
        compiler_params=pltpu.CompilerParams(
            collective_id=0, has_side_effects=True, vmem_limit_bytes=held + (6 << 20)
        ),
    )(*(hbm(x) for x in (local, sign_table)), loss_scale, step_count,
      *(hbm(x) for x in (weights, first_moment, second_moment)))
    out = jax.ShapeDtypeStruct(shape, f32)
    return pl.pallas_call(
        adam_kernel,
        out_shape=(out, out, out),
        in_specs=[vmem] * 6,
        out_specs=(anywhere,) * 3,
        scratch_shapes=[pltpu.VMEM(shape, f32)] * 3 + [dma((3, CHUNKS))],
        compiler_params=pltpu.CompilerParams(vmem_limit_bytes=4 << 20),
    )(*outs)


def solution(mesh):
    own = P("intra", "node")
    return jax.shard_map(
        shards,
        mesh=mesh,
        in_specs=(P("node", "intra", None, None), P(), P(), P(), own, own, own),
        out_specs=(own, own, own),
        check_vma=False,
    )
```

profile of v0, /device:TPU:0, one launch (start us, length us, event | category | flops | bytes accessed | tf_op | source)
XLA Modules:
  0.0 42.4 jit_solution(1694592072276587693)
XLA Ops:
  1.9 39.3 %shard_map.94 = (f32[384,128]{1,0:T(8,128)S(1)}, f32[8,128]{1,0:T(8,128)S(1)}, f32[64,128]{1,0:T(8,128)S(1)}, f32[384,128]{1,0:T(8,128)S(1)}, f32[384,128]{1,0:T(8,128)S(1)}, /*index=5*/f32[384,128]{1,0:T(8,128)S(1)}) custom-call(bf16[3072,512]{1,0:T(8,128)(2,1)} %bitcast.1, s32[64,512]{1,0:T(8,128)} %sign_ref.1, f32[1]{0:T(128)S(6)} %copy.10.scale_ref, ...), custom_call_target="tpu_custom_call" | custom-call | tf_op jit(solution)/shard_map/pallas_call | solution.py:680
  41.2 1.2 %shard_map.95 = (f32[384,128]{1,0:T(8,128)}, f32[384,128]{1,0:T(8,128)}, f32[384,128]{1,0:T(8,128)}) custom-call(f32[384,128]{1,0:T(8,128)S(1)} %get-tuple-element.9.sum_ref, f32[8,128]{1,0:T(8,128)S(1)} %get-tuple-element.10.aux_ref, f32[64,128]{1,0:T(8,128)S(1)} %get-tuple-element.11.sign_ref, f32[384,128]{1,0:T(8,128)S(1)} %get-tuple-element.12.weight_ref, ...), custom_call_target="tpu_custom_call" | custom-call | tf_op jit(solution)/shard_map/pallas_call | solution.py:708
where the time goes:
time: 42.5 us; the launch traced here: 42.4 us
  Pallas kernels  40.5 us (95%)
  between operations  1.93 us (5%)
    pallas_call x1, Pallas kernels, shards(): pl.pallas_call(functools.partial(reduce_kernel, n_node, n_intra), out_sha...  39.3 us
    pallas_call x1, Pallas kernels, shards(): pl.pallas_call(adam_kernel, out_shape=(out, out, out), in_specs=[vmem] *...  1.19 us

commit v1 on v0

--- a/solution.py
+++ b/solution.py
@@ -24,20 +24,14 @@
     return contextlib.nullcontext()
 
 
-def parity_sign(rows, columns):
-    common = lax.broadcasted_iota(jnp.int32, (rows, columns), 0) & lax.broadcasted_iota(
-        jnp.int32, (rows, columns), 1
-    ) & (BLOCK - 1)
-    parity = common
+def parity_sign():
+    shape = (BLOCK, BLOCK)
+    parity = common = lax.broadcasted_iota(jnp.int32, shape, 0) & lax.broadcasted_iota(
+        jnp.int32, shape, 1
+    )
     for bit_index in range(1, BLOCK.bit_length() - 1):
         parity = parity ^ (common >> bit_index)
     return (1 - 2 * (parity & 1)).astype(jnp.float32)
-
-
-def paired_table():
-    row = lax.broadcasted_iota(jnp.int32, (WIDE, WIDE), 0) // BLOCK
-    column = lax.broadcasted_iota(jnp.int32, (WIDE, WIDE), 1) // BLOCK
-    return jnp.where(row == column, parity_sign(WIDE, WIDE), 0.0).astype(jnp.bfloat16)
 
 
 def plan_rows(owned):
@@ -76,9 +70,6 @@
     def at(node_index, z_index, core_index):
         return (node_index, z_index * CORES + core_index)
 
-    def flat(index):
-        return (index // n_intra, index % n_intra)
-
     def send(src, dst, send_sem, recv_sem, device):
         return pltpu.make_async_remote_copy(
             src_ref=src, dst_ref=dst, send_sem=send_sem, recv_sem=recv_sem,
@@ -106,46 +97,62 @@
         ))
     ]
     sides[0].start()
-    for q in range(min(SLOTS, n_intra)):
+    for q in range(CORES):
+        load(q).start()
+
+    barrier = pltpu.get_barrier_semaphore()
+
+    def everyone():
+        for k in range(n_z):
+            p = piece(k)
+            for turn in range(n_node):
+                other = lax.rem(node + turn, n_node)
+                for flip in range(CORES):
+                    if (k, turn, flip) != (last, 0, 0):
+                        yield at(other, p, core if flip == 0 else 1 - core)
+
+    for device in everyone():
+        pl.semaphore_signal(barrier, inc=1, device_id=device, device_id_type=MESH)
+    for q in range(CORES, min(SLOTS, n_intra)):
         load(q).start()
     for copy in sides[1:]:
         copy.start()
-
-    barrier = pltpu.get_barrier_semaphore()
-
-    def greet(step, carry):
-        pl.semaphore_signal(
-            barrier, inc=1, device_id=flat(lax.rem(me + step, n_dev)), device_id_type=MESH
-        )
-        return carry
-
-    lax.fori_loop(1, n_dev, greet, 0)
-    table_bf[...] = paired_table()
+    table = parity_sign().astype(jnp.bfloat16)
+    for a in range(2):
+        for b in range(2):
+            table_bf[a * BLOCK : (a + 1) * BLOCK, b * BLOCK : (b + 1) * BLOCK] = (
+                table if a == b else jnp.zeros_like(table)
+            )
     with scope("Asign"):
         sides[0].wait()
         sign_bf[...] = sign_tab[...].astype(jnp.float32).astype(jnp.bfloat16)
 
-    def rotate(q, most):
-        load(q).wait()
-        i = block_at(q)
-        block = stage[lax.rem(q, SLOTS)]
+    def rotate(m, most):
+        with scope("Aw"):
+            for q in range(CORES):
+                load(m * CORES + q).wait()
+        p = piece(m)
+        blocks = [p * CORES + core, p * CORES + 1 - core]
+        both_blocks = stage[pl.ds(lax.rem(m * CORES, SLOTS), CORES)].reshape(CORES * owned, -1)
         for w in range(n_node // 2):
             cols = slice(w * WIDE, (w + 1) * WIDE)
-            part = block[:, cols].reshape(owned // SIGN_ROWS, SIGN_ROWS, WIDE)
-            signed = (part * sign_bf[:, cols][None]).reshape(owned, WIDE)
+            part = both_blocks[:, cols].reshape(CORES * owned // SIGN_ROWS, SIGN_ROWS, WIDE)
+            signed = (part * sign_bf[:, cols][None]).reshape(CORES * owned, WIDE)
             both = jnp.dot(signed, table_bf[...], preferred_element_type=jnp.float32)
-            for v in range(2):
-                spun = both[:, v * BLOCK : (v + 1) * BLOCK]
-                for h in range(2):
-                    lev[i, w, v, h] = spun[h * half : (h + 1) * half]
-                levz[i, w, v] = spun[2 * half :]
-                most = jnp.maximum(
-                    most, jnp.max(jnp.abs(spun).reshape(owned // 8, 8, BLOCK), axis=0)
-                )
-
-        @pl.when(q + SLOTS < n_intra)
-        def _():
-            load(q + SLOTS).start()
+            for c in range(CORES):
+                for v in range(2):
+                    spun = both[c * owned : (c + 1) * owned, v * BLOCK : (v + 1) * BLOCK]
+                    for h in range(2):
+                        lev[blocks[c], w, v, h] = spun[h * half : (h + 1) * half]
+                    levz[blocks[c], w, v] = spun[2 * half :]
+                    most = jnp.maximum(
+                        most, jnp.max(jnp.abs(spun).reshape(owned // 8, 8, BLOCK), axis=0)
+                    )
+        for q in range(CORES):
+
+            @pl.when(m * CORES + q + SLOTS < n_intra)
+            def _():
+                load(m * CORES + q + SLOTS).start()
 
         return most
 
@@ -214,15 +221,15 @@
             )
         ]
 
-    def third_copy(p, slot, s):
-        r = rows_of(s)
+    def third_copy(p, slot, s, lead=False):
+        r = rows_of(s, lead)
         return send(
             lev.at[p * CORES + core, hi, lo, :, r], third.at[slot, :, r],
             third_send.at[p * SUBS + s], third_recv.at[slot * SUBS + s], at(node, p, core),
         )
 
     def agg_copy(s):
-        r = rows_of(s)
+        r = rows_of(s, True)
         return send(
             lev.at[piece(0) * CORES + core, hi, lo, :, r], agg.at[:, r], agg_send.at[s], agg_recv.at[s],
             at(node, inward, core),
@@ -263,23 +270,22 @@
             )
         ]
 
-    def peak_copy(target, slot):
-        return send(
-            peaks.at[slot], peaks.at[slot], peak_send.at[target], peak_recv.at[slot], flat(target)
-        )
+    def peak_copy(device):
+        return send(peaks.at[me], peaks.at[me], peak_send, peak_recv, device)
+
+    def all_peaks():
+        every = peaks.at[pl.ds(0, n_dev - 1)]
+        return send(every, every, peak_send, peak_recv, at(node, z, 1 - core))
 
     with scope("A_rotate"):
-        most = lax.fori_loop(0, n_intra, rotate, jnp.zeros((8, BLOCK), jnp.float32))
+        most = lax.fori_loop(0, n_z, rotate, jnp.zeros((8, BLOCK), jnp.float32))
         peaks[me] = jnp.max(most, axis=0, keepdims=True)
     with scope("B_barrier"):
         pl.semaphore_wait(barrier, n_dev - 1)
 
-    def tell(step, carry):
-        peak_copy(lax.rem(me + step, n_dev), me).start()
-        return carry
-
     with scope("C_issue"):
-        lax.fori_loop(1, n_dev, tell, 0)
+        for device in everyone():
+            peak_copy(device).start()
         for flip in range(2):
             for copy in raw_copies(flip):
                 copy.start()
@@ -304,13 +310,8 @@
         aux_ref[0:1] = 1.0 / (1.0 - jnp.exp(steps * math.log(0.9)))
         aux_ref[1:2] = 1.0 / (1.0 - jnp.exp(steps * math.log(0.95)))
 
-    def hear(step, carry):
-        other = lax.rem(me + step, n_dev)
-        peak_copy(other, other).wait_recv()
-        return carry
-
     with scope("E_peaks"):
-        lax.fori_loop(1, n_dev, hear, 0)
+        all_peaks().wait_recv()
         tops = jnp.max(peaks[...], axis=0)
         top_value = jnp.max(tops, axis=1, keepdims=True) * ROOT
         level_scale = 127.0 / top_value
@@ -430,32 +431,6 @@
                 z_level(p, h, h == 0)
                 z_copy(p, h).start()
 
-    with scope("F0"):
-        level_piece(0, 1, True)
-        z_lead()
-        level_piece(1, 0)
-        z_ahead(1)
-        raw_piece()
-    with scope("F1"):
-        z_inner(0, 1)
-        level_piece(1, 1)
-        z_ahead(2)
-        first_sum(0, 1, True)
-        second_sum(0, 0, True)
-        z_inner(1, 0)
-        first_sum(1, 0)
-        second_sum(0, 1, True)
-
-        @pl.when(end)
-        def _():
-            for s in range(SUBS):
-                agg_copy(s).start()
-
-        @pl.when(jnp.logical_not(end | near))
-        def _():
-            for s in range(SUBS):
-                third_copy(piece(0), z, s).start()
-
     def z_finish():
         for h in range(2):
             z_level(z, h, h == 0)
@@ -471,51 +446,7 @@
         for copy in z_first_copies():
             copy.start()
 
-    def pipeline(k, carry):
-        for s in range(SUBS):
-            with scope("G%d" % s):
-                level_piece(k, s)
-                z_ahead(1 + (k - 1) * SUBS + s)
-                if s == 0:
-                    first_sum(k - 1, 1)
-
-                    @pl.when(k < last)
-                    def _():
-                        z_inner(k - 1, 1)
-
-                    @pl.when((k == last) & near)
-                    def _():
-                        p = piece(0)
-                        i = p * CORES + core
-                        for part in range(SUBS):
-                            r = rows_of(part)
-                            agg_copy(part).wait_recv()
-                            for h in range(2):
-                                lev[i, hi, lo, h, r] = lev[i, hi, lo, h, r] + agg[h, r]
-                            third_copy(p, z, part).start()
-                else:
-                    first_sum(k, 0)
-
-                    @pl.when(k < last)
-                    def _():
-                        z_inner(k, 0)
-
-                    @pl.when(k == last - 1)
-                    def _():
-                        z_inner(k, 1)
-
-                with scope("Gs"):
-                    second_sum(k - 1, s)
-                third_copy(piece(k - 1), z, s).start()
-        return carry
-
-    lax.fori_loop(2, n_z, pipeline, 0)
-    with scope("H_zfinal"):
-        z_finish()
-    with scope("I_tail"):
-        first_sum(last, 1)
-        second_sum(last, 0)
-    with scope("J_ztail"):
+    def z_relay():
         for copy in z_first_copies():
             copy.wait_recv()
         for j in range(2):
@@ -523,19 +454,98 @@
             levz[intra, hi, j, z_part(1)] = levz[intra, hi, j, z_part(1)] + zfirst[1, j]
         for copy in z_second_copies():
             copy.start()
+
+    def lead_third(s):
+        second_sum(0, s, True)
+
+        @pl.when(end)
+        def _():
+            agg_copy(s).start()
+
+        @pl.when(jnp.logical_not(end | near))
+        def _():
+            third_copy(piece(0), z, s, True).start()
+
+    def near_third(k, s):
+        @pl.when(near & (k == 2))
+        def _():
+            p = piece(0)
+            i, r = p * CORES + core, rows_of(s, True)
+            agg_copy(s).wait_recv()
+            for h in range(2):
+                lev[i, hi, lo, h, r] = lev[i, hi, lo, h, r] + agg[h, r]
+            third_copy(p, z, s, True).start()
+
+    def advance(k, is_first=False, is_last=False):
+        for s in range(SUBS):
+            with scope("G%d" % s):
+                if not is_last:
+                    level_piece(k + 1, s)
+                    z_ahead(1 + k * SUBS + s)
+                if not (is_first or is_last):
+                    z_inner(k, s)
+                with scope("Gf"):
+                    first_sum(k, s)
+                if is_first:
+                    with scope("Gz"):
+                        z_inner(k, s)
+                if is_last:
+                    with scope("Gz"):
+                        if s == 0:
+                            z_finish()
+                        else:
+                            z_relay()
+                with scope("Gs"):
+                    if is_first:
+                        lead_third(s)
+                        if s == 0:
+                            z_ahead(2)
+                    elif not is_last:
+                        near_third(k, s)
+                    if s == 0 and not is_first:
+                        second_sum(k - 1, 1)
+                        third_copy(piece(k - 1), z, 1).start()
+                    elif s == 1:
+                        second_sum(k, 0)
+                        if not is_last:
+                            third_copy(piece(k), z, 0).start()
+
+    def middle(k, carry):
+        advance(k)
+        return carry
+
+    with scope("F0"):
+        level_piece(0, 1, True)
+        z_lead()
+        level_piece(1, 0)
+        z_ahead(1)
+        with scope("Fr"):
+            raw_piece()
+        level_piece(1, 1)
+    with scope("F1"):
+        with scope("Fz"):
+            z_inner(0, 1)
+        first_sum(0, 1, True)
+    advance(1, is_first=True)
+    lax.fori_loop(2, last, middle, 0)
+    advance(last, is_last=True)
     with scope("K_last"):
         second_sum(last, 1)
 
     def from_plane(step, carry):
         other = lax.rem(z + step, n_z)
 
-        @pl.when(jnp.abs(other - z) != last)
-        def _():
+        def take(lead):
             for s in range(SUBS):
-                r = rows_of(s)
-                third_copy(other, other, s).wait_recv()
+                r = rows_of(s, lead)
+                third_copy(other, other, s, lead).wait_recv()
                 for h in range(2):
                     lev[intra, hi, lo, h, r] = lev[intra, hi, lo, h, r] + third[other, h, r]
+
+        lead = ((z == last) & (other < n_z // 2)) | ((z == 0) & (other >= n_z // 2))
+        agged = jnp.abs(other - z) == last
+        pl.when(lead & jnp.logical_not(agged))(lambda: take(True))
+        pl.when(jnp.logical_not(lead | agged))(lambda: take(False))
 
         return carry
 
@@ -551,10 +561,6 @@
                 levz[intra, hi, lo, z_part(h)] + zsecond[h]
             )
 
-    def told(step, carry):
-        peak_copy(lax.rem(me + step, n_dev), me).wait_send()
-        return carry
-
     def finish(k, carry):
         p = piece(k)
         pair_copy(p).wait_send()
@@ -573,13 +579,21 @@
         @pl.when((k < last) & jnp.logical_not(end & (k == 0)))
         def _():
             z_copy(p, 0).wait_send()
+
+        @pl.when((k == 0) & jnp.logical_not(end))
+        def _():
+            for s in range(SUBS):
+                third_copy(p, z, s, True).wait_send()
+
+        @pl.when((k > 0) & (k < last))
+        def _():
             for s in range(SUBS):
                 third_copy(p, z, s).wait_send()
 
         return carry
 
     with scope("N_finish"):
-        lax.fori_loop(1, n_dev, told, 0)
+        all_peaks().wait_send()
         for flip in range(2):
             for copy in raw_copies(flip):
                 copy.wait_send()
@@ -604,9 +618,8 @@
     new_weight_ref, new_first_ref, new_second_ref, weight_buf, first_buf, second_buf, sems,
 ):
     owned = sum_ref.shape[0]
-    table = parity_sign(WIDE, BLOCK)
-    upper = lax.broadcasted_iota(jnp.int32, (WIDE, BLOCK), 0) < BLOCK
-    table = jnp.where(upper, table * 64.0, table).astype(jnp.bfloat16)
+    table = parity_sign()
+    table = jnp.concatenate([table * 64.0, table], axis=0).astype(jnp.bfloat16)
     signs = sign_ref[...]
     first_unbias, second_unbias = aux_ref[0:1], aux_ref[1:2]
     rows = owned // CHUNKS
@@ -697,7 +710,7 @@
             dma((SUBS,)), dma((SUBS,)),
             dma((n_z * 2,)), dma((n_z * 2 + 2,)),
             dma((2,)), dma((2,)), dma((2,)), dma((2,)),
-            dma((n_dev,)), dma((n_dev,)),
+            dma, dma,
         ],
         compiler_params=pltpu.CompilerParams(
             collective_id=0, has_side_effects=True, vmem_limit_bytes=held + (6 << 20)

time: 42.5 us -> 39.8 us (0.936)
  Pallas kernels: 40.5 us -> 37.7 us
    pallas_call x1, Pallas kernels: 39.3 us -> 36.6 us  [shards(): pl.pallas_call(functools.partial(reduce_kernel, n_node, n_intra), out_sha...]
where the time goes in v1:
time: 39.8 us; the launch traced here: 39.7 us
  Pallas kernels  37.7 us (95%)
  between operations  1.93 us (5%)
    pallas_call x1, Pallas kernels, shards(): pl.pallas_call(functools.partial(reduce_kernel, n_node, n_intra), out_sha...  36.6 us
    pallas_call x1, Pallas kernels, shards(): pl.pallas_call(adam_kernel, out_shape=(out, out, out), in_specs=[vmem] *...  1.14 us

profile of v1, /device:TPU:0, one launch (start us, length us, event | category | flops | bytes accessed | tf_op | source)
XLA Modules:
  0.0 39.7 jit_solution(7326205697742025241)
XLA Ops:
  1.9 36.6 %shard_map.94 = (f32[384,128]{1,0:T(8,128)S(1)}, f32[8,128]{1,0:T(8,128)S(1)}, f32[64,128]{1,0:T(8,128)S(1)}, f32[384,128]{1,0:T(8,128)S(1)}, f32[384,128]{1,0:T(8,128)S(1)}, /*index=5*/f32[384,128]{1,0:T(8,128)S(1)}) custom-call(bf16[3072,512]{1,0:T(8,128)(2,1)} %bitcast.1, s32[64,512]{1,0:T(8,128)} %sign_ref.1, f32[1]{0:T(128)S(6)} %copy.10.scale_ref, ...), custom_call_target="tpu_custom_call" | custom-call | tf_op jit(solution)/shard_map/pallas_call | solution.py:693
  38.5 1.1 %shard_map.95 = (f32[384,128]{1,0:T(8,128)}, f32[384,128]{1,0:T(8,128)}, f32[384,128]{1,0:T(8,128)}) custom-call(f32[384,128]{1,0:T(8,128)S(1)} %get-tuple-element.9.sum_ref, f32[8,128]{1,0:T(8,128)S(1)} %get-tuple-element.10.aux_ref, f32[64,128]{1,0:T(8,128)S(1)} %get-tuple-element.11.sign_ref, f32[384,128]{1,0:T(8,128)S(1)} %get-tuple-element.12.weight_ref, ...), custom_call_target="tpu_custom_call" | custom-call | tf_op jit(solution)/shard_map/pallas_call | solution.py:721

commit v2 on v1

--- a/solution.py
+++ b/solution.py
@@ -35,7 +35,7 @@
 
 
 def plan_rows(owned):
-    z_rows = owned * 5 // 24 // 16 * 16
+    z_rows = owned // 4 // 16 * 16
     return z_rows, (owned - z_rows) // 2
 
 
@@ -57,7 +57,7 @@
     zh = z_rows // 2
     cut = (half // SUBS + 7) // 8 * 8
     spans = ((0, cut), (cut, half - cut))
-    raw_rows = half * 7 // 10 // 8 * 8
+    raw_rows = half * 8 // 10 // 8 * 8
     raw_spans = ((0, raw_rows), (raw_rows, half - raw_rows))
     node, intra = lax.axis_index("node"), lax.axis_index("intra")
     z, core = intra // CORES, intra % CORES
@@ -128,9 +128,8 @@
         sign_bf[...] = sign_tab[...].astype(jnp.float32).astype(jnp.bfloat16)
 
     def rotate(m, most):
-        with scope("Aw"):
-            for q in range(CORES):
-                load(m * CORES + q).wait()
+        for q in range(CORES):
+            load(m * CORES + q).wait()
         p = piece(m)
         blocks = [p * CORES + core, p * CORES + 1 - core]
         both_blocks = stage[pl.ds(lax.rem(m * CORES, SLOTS), CORES)].reshape(CORES * owned, -1)
@@ -228,11 +227,11 @@
             third_send.at[p * SUBS + s], third_recv.at[slot * SUBS + s], at(node, p, core),
         )
 
-    def agg_copy(s):
-        r = rows_of(s, True)
+    def agg_copy(k, s, lead=False):
+        r = rows_of(s, lead)
         return send(
-            lev.at[piece(0) * CORES + core, hi, lo, :, r], agg.at[:, r], agg_send.at[s], agg_recv.at[s],
-            at(node, inward, core),
+            lev.at[piece(k) * CORES + core, hi, lo, :, r], agg.at[k, :, r],
+            agg_send.at[k * SUBS + s], agg_recv.at[k * SUBS + s], at(node, inward, core),
         )
 
     def z_part(h):
@@ -423,13 +422,12 @@
         def _():
             z_pass(0, 0)
 
-    def z_ahead(k):
+    def z_ahead(k, h):
         @pl.when(end & (k < last))
         def _():
             p = piece(k)
-            for h in range(2):
-                z_level(p, h, h == 0)
-                z_copy(p, h).start()
+            z_level(p, h, h == 0)
+            z_copy(p, h).start()
 
     def z_finish():
         for h in range(2):
@@ -455,70 +453,88 @@
         for copy in z_second_copies():
             copy.start()
 
-    def lead_third(s):
-        second_sum(0, s, True)
-
-        @pl.when(end)
-        def _():
-            agg_copy(s).start()
-
-        @pl.when(jnp.logical_not(end | near))
-        def _():
-            third_copy(piece(0), z, s, True).start()
-
-    def near_third(k, s):
-        @pl.when(near & (k == 2))
-        def _():
-            p = piece(0)
-            i, r = p * CORES + core, rows_of(s, True)
-            agg_copy(s).wait_recv()
+    def give_third(k, s, lead=False):
+        p = piece(k)
+        second_sum(k, s, lead)
+        via = k <= last - 2
+
+        @pl.when(end & via)
+        def _():
+            agg_copy(k, s, lead).start()
+
+        @pl.when(jnp.logical_not((end | near) & via))
+        def _():
+            third_copy(p, z, s, lead).start()
+
+    def near_third(k, s, lead=False):
+        @pl.when(near)
+        def _():
+            p = piece(k)
+            i, r = p * CORES + core, rows_of(s, lead)
+            agg_copy(k, s, lead).wait_recv()
             for h in range(2):
-                lev[i, hi, lo, h, r] = lev[i, hi, lo, h, r] + agg[h, r]
-            third_copy(p, z, s, True).start()
-
-    def advance(k, is_first=False, is_last=False):
-        for s in range(SUBS):
-            with scope("G%d" % s):
-                if not is_last:
-                    level_piece(k + 1, s)
-                    z_ahead(1 + k * SUBS + s)
-                if not (is_first or is_last):
-                    z_inner(k, s)
-                with scope("Gf"):
-                    first_sum(k, s)
-                if is_first:
-                    with scope("Gz"):
-                        z_inner(k, s)
-                if is_last:
-                    with scope("Gz"):
-                        if s == 0:
-                            z_finish()
-                        else:
-                            z_relay()
-                with scope("Gs"):
-                    if is_first:
-                        lead_third(s)
-                        if s == 0:
-                            z_ahead(2)
-                    elif not is_last:
-                        near_third(k, s)
-                    if s == 0 and not is_first:
-                        second_sum(k - 1, 1)
-                        third_copy(piece(k - 1), z, 1).start()
-                    elif s == 1:
-                        second_sum(k, 0)
-                        if not is_last:
-                            third_copy(piece(k), z, 0).start()
+                lev[i, hi, lo, h, r] = lev[i, hi, lo, h, r] + agg[k, h, r]
+            third_copy(p, z, s, lead).start()
+
+    def begin():
+        with scope("G0"):
+            first_sum(1, 0)
+            level_piece(2, 1)
+            with scope("Gz"):
+                z_inner(1, 0)
+                z_inner(2, 0)
+            z_ahead(2, 0)
+            with scope("Gs"):
+                give_third(0, 0, True)
+            z_ahead(2, 1)
+        with scope("G1"):
+            first_sum(1, 1)
+            level_piece(3, 0)
+            with scope("Gz"):
+                z_inner(1, 1)
+                z_inner(2, 1)
+            with scope("Gn"):
+                near_third(0, 0, True)
+            with scope("Gs"):
+                give_third(0, 1, True)
+            with scope("Gs"):
+                give_third(1, 0)
 
     def middle(k, carry):
-        advance(k)
+        with scope("M0"):
+            first_sum(k, 0)
+        with scope("M1"):
+            first_sum(k, 1)
+        level_piece(k + 1, 1)
+        pl.when(k + 2 <= last)(lambda: level_piece(k + 2, 0))
+        for h in range(2):
+            z_ahead(k + 1, h)
+            pl.when(k + 1 < last)(lambda: z_inner(k + 1, h))
+        with scope("M2"):
+            give_third(k - 1, 1)
+        with scope("Mz"):
+            pl.when(k == last - 1)(z_finish)
+        with scope("M3"):
+
+            @pl.when(k == 2)
+            def _():
+                near_third(0, 1, True)
+
+            @pl.when(k > 2)
+            def _():
+                for s in range(SUBS):
+                    near_third(k - 2, s)
+
+        with scope("M4"):
+            give_third(k, 0)
         return carry
 
     with scope("F0"):
         level_piece(0, 1, True)
         z_lead()
         level_piece(1, 0)
-        z_ahead(1)
+        for h in range(2):
+            z_ahead(1, h)
         with scope("Fr"):
             raw_piece()
         level_piece(1, 1)
@@ -526,10 +542,23 @@
         with scope("Fz"):
             z_inner(0, 1)
         first_sum(0, 1, True)
-    advance(1, is_first=True)
+        level_piece(2, 0)
+    begin()
     lax.fori_loop(2, last, middle, 0)
-    advance(last, is_last=True)
-    with scope("K_last"):
+    with scope("H0"):
+        first_sum(last, 0)
+    with scope("H1"):
+        give_third(last - 1, 1)
+    with scope("H2"):
+        for s in range(SUBS):
+            near_third(last - 2, s)
+    with scope("H3"):
+        first_sum(last, 1)
+    with scope("H4"):
+        z_relay()
+    with scope("K0"):
+        second_sum(last, 0)
+    with scope("K1"):
         second_sum(last, 1)
 
     def from_plane(step, carry):
@@ -543,7 +572,7 @@
                     lev[intra, hi, lo, h, r] = lev[intra, hi, lo, h, r] + third[other, h, r]
 
         lead = ((z == last) & (other < n_z // 2)) | ((z == 0) & (other >= n_z // 2))
-        agged = jnp.abs(other - z) == last
+        agged = ((other == 0) | (other == last)) & (jnp.abs(other - z) > 1)
         pl.when(lead & jnp.logical_not(agged))(lambda: take(True))
         pl.when(jnp.logical_not(lead | agged))(lambda: take(False))
 
@@ -580,15 +609,14 @@
         def _():
             z_copy(p, 0).wait_send()
 
-        @pl.when((k == 0) & jnp.logical_not(end))
-        def _():
+        def gave(lead):
+            via = end & (k <= last - 2)
             for s in range(SUBS):
-                third_copy(p, z, s, True).wait_send()
-
-        @pl.when((k > 0) & (k < last))
-        def _():
-            for s in range(SUBS):
-                third_copy(p, z, s).wait_send()
+                pl.when(via)(lambda: agg_copy(k, s, lead).wait_send())
+                pl.when(jnp.logical_not(via))(lambda: third_copy(p, z, s, lead).wait_send())
+
+        pl.when(k == 0)(lambda: gave(True))
+        pl.when((k > 0) & (k < last))(lambda: gave(False))
 
         return carry
 
@@ -605,8 +633,6 @@
         def _():
             for flip in range(2):
                 zraw_copy(flip).wait_send()
-            for s in range(SUBS):
-                agg_copy(s).wait_send()
 
         lax.fori_loop(0, n_z, finish, 0)
         for copy in z_first_copies() + z_second_copies():
@@ -677,12 +703,12 @@
         ((n_intra, n_hi, 2, z_rows, BLOCK), f32),
         ((n_z, n_hi, 2, 2, half, BLOCK), f32),
         ((n_z, n_hi, 2, z_rows, BLOCK), f32),
-        ((2, 2, 2, half * 7 // 10 // 8 * 8, BLOCK), f32),
+        ((2, 2, 2, half * 8 // 10 // 8 * 8, BLOCK), f32),
         ((2, n_hi, 2, zh, BLOCK), f32),
         ((n_z, 2, 2, half, BLOCK), f32),
         ((n_z, 2, half, BLOCK), f32),
         ((n_z, 2, half, BLOCK), f32),
-        ((2, half, BLOCK), f32),
+        ((n_z - 2, 2, half, BLOCK), f32),
         ((n_z + 1, n_hi, 2, z_rows, BLOCK), f32),
         ((2, 2, zh, BLOCK), f32),
         ((2, zh, BLOCK), f32),
@@ -707,7 +733,7 @@
             dma((2, n_z * SUBS)), dma((2, n_z * SUBS)),
             dma((2, n_z * SUBS)), dma((2, n_z * SUBS)),
             dma((n_z * SUBS,)), dma((n_z * SUBS,)),
-            dma((SUBS,)), dma((SUBS,)),
+            dma(((n_z - 2) * SUBS,)), dma(((n_z - 2) * SUBS,)),
             dma((n_z * 2,)), dma((n_z * 2 + 2,)),
             dma((2,)), dma((2,)), dma((2,)), dma((2,)),
             dma, dma,

time: 39.8 us -> 37.9 us (0.952)
  Pallas kernels: 37.7 us -> 35.8 us
    pallas_call x1, Pallas kernels: 36.6 us -> 34.6 us  [shards(): pl.pallas_call(functools.partial(reduce_kernel, n_node, n_intra), out_sha...]
where the time goes in v2:
time: 37.9 us; the launch traced here: 37.7 us
  Pallas kernels  35.8 us (94%)
  between operations  1.93 us (5%)
    pallas_call x1, Pallas kernels, shards(): pl.pallas_call(functools.partial(reduce_kernel, n_node, n_intra), out_sha...  34.6 us
    pallas_call x1, Pallas kernels, shards(): pl.pallas_call(adam_kernel, out_shape=(out, out, out), in_specs=[vmem] *...  1.14 us

profile of v2, /device:TPU:0, one launch (start us, length us, event | category | flops | bytes accessed | tf_op | source)
XLA Modules:
  0.0 37.7 jit_solution(14000415222060584399)
XLA Ops:
  1.9 34.6 %shard_map.94 = (f32[384,128]{1,0:T(8,128)S(1)}, f32[8,128]{1,0:T(8,128)S(1)}, f32[64,128]{1,0:T(8,128)S(1)}, f32[384,128]{1,0:T(8,128)S(1)}, f32[384,128]{1,0:T(8,128)S(1)}, /*index=5*/f32[384,128]{1,0:T(8,128)S(1)}) custom-call(bf16[3072,512]{1,0:T(8,128)(2,1)} %bitcast.1, s32[64,512]{1,0:T(8,128)} %sign_ref.1, f32[1]{0:T(128)S(6)} %copy.10.scale_ref, ...), custom_call_target="tpu_custom_call" | custom-call | tf_op jit(solution)/shard_map/pallas_call | solution.py:719
  36.6 1.1 %shard_map.95 = (f32[384,128]{1,0:T(8,128)}, f32[384,128]{1,0:T(8,128)}, f32[384,128]{1,0:T(8,128)}) custom-call(f32[384,128]{1,0:T(8,128)S(1)} %get-tuple-element.9.sum_ref, f32[8,128]{1,0:T(8,128)S(1)} %get-tuple-element.10.aux_ref, f32[64,128]{1,0:T(8,128)S(1)} %get-tuple-element.11.sign_ref, f32[384,128]{1,0:T(8,128)S(1)} %get-tuple-element.12.weight_ref, ...), custom_call_target="tpu_custom_call" | custom-call | tf_op jit(solution)/shard_map/pallas_call | solution.py:747

commit v3 on v2

--- a/solution.py
+++ b/solution.py
@@ -15,7 +15,6 @@
 CORES = 2
 SLOTS = 8
 SUBS = 2
-CHUNKS = 3
 ROOT = 1.0 / math.sqrt(BLOCK)
 MESH = pl.DeviceIdType.MESH
 
@@ -41,8 +40,8 @@
 
 def reduce_kernel(
     n_node, n_intra, grad_ref, sign_ref, scale_ref, step_ref, weight_ref, first_ref, second_ref,
-    sum_ref, aux_ref, sign_out, weight_out, first_out, second_out,
-    stage, sign_tab, sign_bf, table_bf, lev, levz, pair, pairz, raw, zraw, first, second, third, agg,
+    new_weight_ref, new_first_ref, new_second_ref,
+    stage, sign_tab, sign_bf, table_bf, split_bf, sign_own, weight_in, first_in, second_in, lev, levz, pair, pairz, raw, zraw, first, second, third, agg,
     zin, zfirst, zsecond, peaks,
     load_sem, side_sem, pair_send, pair_recv, pairz_send, pairz_recv, raw_send, raw_recv,
     zraw_send, zraw_recv, first_send, first_recv, second_send, second_recv, third_send, third_recv,
@@ -52,7 +51,7 @@
     n_z = n_intra // CORES
     last = n_z - 1
     n_dev = n_node * n_intra
-    owned = sum_ref.shape[0]
+    owned = new_weight_ref.shape[0]
     z_rows, half = plan_rows(owned)
     zh = z_rows // 2
     cut = (half // SUBS + 7) // 8 * 8
@@ -93,7 +92,7 @@
     sides = [
         pltpu.make_async_copy(src, dst, side_sem.at[n])
         for n, (src, dst) in enumerate((
-            (sign_ref, sign_tab), (weight_ref, weight_out), (first_ref, first_out), (second_ref, second_out),
+            (sign_ref, sign_tab), (weight_ref, weight_in), (first_ref, first_in), (second_ref, second_in),
         ))
     ]
     sides[0].start()
@@ -306,17 +305,16 @@
             copy.wait()
         ones = jnp.ones((1, BLOCK), jnp.float32)
         steps = ones * step_ref[0].astype(jnp.float32)
-        aux_ref[0:1] = 1.0 / (1.0 - jnp.exp(steps * math.log(0.9)))
-        aux_ref[1:2] = 1.0 / (1.0 - jnp.exp(steps * math.log(0.95)))
+        first_unbias = 1.0 / (1.0 - jnp.exp(steps * math.log(0.9)))
+        second_unbias = 1.0 / (1.0 - jnp.exp(steps * math.log(0.95)))
+        split_bf[0:BLOCK] = (parity_sign() * 64.0).astype(jnp.bfloat16)
+        split_bf[BLOCK:] = parity_sign().astype(jnp.bfloat16)
 
     with scope("E_peaks"):
         all_peaks().wait_recv()
         tops = jnp.max(peaks[...], axis=0)
         top_value = jnp.max(tops, axis=1, keepdims=True) * ROOT
         level_scale = 127.0 / top_value
-        factor = (ones * top_value) / (ones * (127.0 * float(n_dev) * scale_ref[0]))
-        column = pl.multiple_of(node * BLOCK, BLOCK)
-        sign_out[...] = sign_tab[:, pl.ds(column, BLOCK)].astype(jnp.float32) * (factor * ROOT)
 
     def level(value):
         return jnp.floor((value * ROOT) * level_scale + 0.5)
@@ -493,8 +491,6 @@
             with scope("Gz"):
                 z_inner(1, 1)
                 z_inner(2, 1)
-            with scope("Gn"):
-                near_third(0, 0, True)
             with scope("Gs"):
                 give_third(0, 1, True)
             with scope("Gs"):
@@ -510,21 +506,22 @@
         for h in range(2):
             z_ahead(k + 1, h)
             pl.when(k + 1 < last)(lambda: z_inner(k + 1, h))
+        with scope("M3"):
+
+            @pl.when(k == 2)
+            def _():
+                for s in range(SUBS):
+                    near_third(0, s, True)
+
+            @pl.when(k > 2)
+            def _():
+                for s in range(SUBS):
+                    near_third(k - 2, s)
+
         with scope("M2"):
             give_third(k - 1, 1)
         with scope("Mz"):
             pl.when(k == last - 1)(z_finish)
-        with scope("M3"):
-
-            @pl.when(k == 2)
-            def _():
-                near_third(0, 1, True)
-
-            @pl.when(k > 2)
-            def _():
-                for s in range(SUBS):
-                    near_third(k - 2, s)
-
         with scope("M4"):
             give_third(k, 0)
         return carry
@@ -544,16 +541,21 @@
         first_sum(0, 1, True)
         level_piece(2, 0)
     begin()
+    factor = (ones * top_value) / (ones * (127.0 * float(n_dev) * scale_ref[0]))
+    column = pl.multiple_of(node * BLOCK, BLOCK)
+    own_signs = sign_tab[:, pl.ds(column, BLOCK)].astype(jnp.float32) * (factor * ROOT)
+    for n in range(owned // SIGN_ROWS):
+        sign_own[n * SIGN_ROWS : (n + 1) * SIGN_ROWS] = own_signs
     lax.fori_loop(2, last, middle, 0)
     with scope("H0"):
         first_sum(last, 0)
     with scope("H1"):
         give_third(last - 1, 1)
+    with scope("H3"):
+        first_sum(last, 1)
     with scope("H2"):
         for s in range(SUBS):
             near_third(last - 2, s)
-    with scope("H3"):
-        first_sum(last, 1)
     with scope("H4"):
         z_relay()
     with scope("K0"):
@@ -561,34 +563,62 @@
     with scope("K1"):
         second_sum(last, 1)
 
+    def adam(start, summed):
+        r = pl.ds(start, summed.shape[0])
+        high = jnp.floor(summed * (1.0 / 64.0))
+        low = summed - high * 64.0
+        both = jnp.concatenate([high, low], axis=1).astype(jnp.bfloat16)
+        grad = jnp.dot(both, split_bf[...], preferred_element_type=jnp.float32) * sign_own[r]
+        new_first = 0.9 * first_in[r] + 0.1 * grad
+        new_second = 0.95 * second_in[r] + 0.05 * grad * grad
+        new_first_ref[r] = new_first
+        new_second_ref[r] = new_second
+        weights = weight_in[r]
+        update = (new_first * first_unbias) / (jnp.sqrt(new_second * second_unbias) + 1e-08)
+        new_weight_ref[r] = weights - 0.2 * (update + 0.1 * weights)
+
+    def is_lead(other):
+        return ((z == last) & (other < n_z // 2)) | ((z == 0) & (other >= n_z // 2))
+
+    def direct(other):
+        return jnp.logical_not(((other == 0) | (other == last)) & (jnp.abs(other - z) > 1))
+
     def from_plane(step, carry):
         other = lax.rem(z + step, n_z)
-
-        def take(lead):
-            for s in range(SUBS):
-                r = rows_of(s, lead)
-                third_copy(other, other, s, lead).wait_recv()
-                for h in range(2):
-                    lev[intra, hi, lo, h, r] = lev[intra, hi, lo, h, r] + third[other, h, r]
-
-        lead = ((z == last) & (other < n_z // 2)) | ((z == 0) & (other >= n_z // 2))
-        agged = ((other == 0) | (other == last)) & (jnp.abs(other - z) > 1)
-        pl.when(lead & jnp.logical_not(agged))(lambda: take(True))
-        pl.when(jnp.logical_not(lead | agged))(lambda: take(False))
+        for s in range(SUBS):
+            for lead in (False, True):
+
+                @pl.when(direct(other) & (is_lead(other) == lead))
+                def _():
+                    third_copy(other, other, s, lead).wait_recv()
+
+        return carry
+
+    def add_plane(step, carry):
+        other = lax.rem(z + step, n_z)
+
+        @pl.when(direct(other))
+        def _():
+            lev[intra, hi, lo] = lev[intra, hi, lo] + third[other]
 
         return carry
 
     with scope("L_third"):
         lax.fori_loop(1, n_z, from_plane, 0)
+        lax.fori_loop(1, n_z, add_plane, 0)
+    with scope("L_adam"):
         for h in range(2):
-            sum_ref[h * half : (h + 1) * half] = lev[intra, hi, lo, h]
+            adam(h * half, lev[intra, hi, lo, h])
     with scope("M_zlast"):
         for copy in z_second_copies():
             copy.wait_recv()
-        for h in range(2):
-            sum_ref[2 * half + h * zh : 2 * half + (h + 1) * zh] = (
-                levz[intra, hi, lo, z_part(h)] + zsecond[h]
-            )
+    with scope("M_adam"):
+        adam(
+            2 * half,
+            jnp.concatenate(
+                [levz[intra, hi, lo, z_part(h)] + zsecond[h] for h in range(2)], axis=0
+            ),
+        )
 
     def finish(k, carry):
         p = piece(k)
@@ -639,38 +669,11 @@
             copy.wait_send()
 
 
-def adam_kernel(
-    sum_ref, aux_ref, sign_ref, weight_ref, first_ref, second_ref,
-    new_weight_ref, new_first_ref, new_second_ref, weight_buf, first_buf, second_buf, sems,
-):
-    owned = sum_ref.shape[0]
-    table = parity_sign()
-    table = jnp.concatenate([table * 64.0, table], axis=0).astype(jnp.bfloat16)
-    signs = sign_ref[...]
-    first_unbias, second_unbias = aux_ref[0:1], aux_ref[1:2]
-    rows = owned // CHUNKS
-    copies = []
-    for c in range(CHUNKS):
-        r = slice(c * rows, (c + 1) * rows)
-        summed = sum_ref[r]
-        high = jnp.floor(summed * (1.0 / 64.0))
-        low = summed - high * 64.0
-        both = jnp.concatenate([high, low], axis=1).astype(jnp.bfloat16)
-        back = jnp.dot(both, table, preferred_element_type=jnp.float32)
-        grad = (back.reshape(rows // SIGN_ROWS, SIGN_ROWS, BLOCK) * signs[None]).reshape(rows, BLOCK)
-        new_first = 0.9 * first_ref[r] + 0.1 * grad
-        new_second = 0.95 * second_ref[r] + 0.05 * grad * grad
-        first_buf[r] = new_first
-        second_buf[r] = new_second
-        weights = weight_ref[r]
-        update = (new_first * first_unbias) / (jnp.sqrt(new_second * second_unbias) + 1e-08)
-        weight_buf[r] = weights - 0.2 * (update + 0.1 * weights)
-        for n, (src, dst) in enumerate((
-            (first_buf, new_first_ref), (second_buf, new_second_ref), (weight_buf, new_weight_ref),
-        )):
-            copy = pltpu.make_async_copy(src.at[r], dst.at[r], sems.at[n, c])
-            copy.start()
-            copies.append(copy)
+def store_kernel(*refs):
+    sems = refs[-1]
+    copies = [pltpu.make_async_copy(refs[n], refs[n + 3], sems.at[n]) for n in range(3)]
+    for copy in copies:
+        copy.start()
     for copy in copies:
         copy.wait()
 
@@ -697,7 +700,8 @@
         ((SIGN_ROWS, columns), jnp.int32),
         ((SIGN_ROWS, columns), jnp.bfloat16),
         ((WIDE, WIDE), jnp.bfloat16),
-    ]
+        ((WIDE, BLOCK), jnp.bfloat16),
+    ] + [((owned, BLOCK), f32)] * 4
     large = [
         ((n_intra, n_hi, 2, 2, half, BLOCK), f32),
         ((n_intra, n_hi, 2, z_rows, BLOCK), f32),
@@ -718,12 +722,9 @@
     shape = (owned, BLOCK)
     outs = pl.pallas_call(
         functools.partial(reduce_kernel, n_node, n_intra),
-        out_shape=(
-            pltpu.VMEM(shape, f32), pltpu.VMEM((8, BLOCK), f32), pltpu.VMEM((SIGN_ROWS, BLOCK), f32),
-            pltpu.VMEM(shape, f32), pltpu.VMEM(shape, f32), pltpu.VMEM(shape, f32),
-        ),
+        out_shape=(pltpu.VMEM(shape, f32),) * 3,
         in_specs=[anywhere] * 2 + [smem] * 2 + [anywhere] * 3,
-        out_specs=(vmem,) * 6,
+        out_specs=(vmem,) * 3,
         scratch_shapes=[pltpu.VMEM(*b) for b in buffers]
         + [pltpu.VMEM(*b) for b in large]
         + [
@@ -745,12 +746,12 @@
       *(hbm(x) for x in (weights, first_moment, second_moment)))
     out = jax.ShapeDtypeStruct(shape, f32)
     return pl.pallas_call(
-        adam_kernel,
+        store_kernel,
         out_shape=(out, out, out),
-        in_specs=[vmem] * 6,
+        in_specs=[vmem] * 3,
         out_specs=(anywhere,) * 3,
-        scratch_shapes=[pltpu.VMEM(shape, f32)] * 3 + [dma((3, CHUNKS))],
-        compiler_params=pltpu.CompilerParams(vmem_limit_bytes=4 << 20),
+        scratch_shapes=[dma((3,))],
+        compiler_params=pltpu.CompilerParams(vmem_limit_bytes=1 << 20),
     )(*outs)
 
 

time: 37.9 us -> 37.8 us (level)
  no operation moved by 1% of the time
where the time goes in v3:
time: 37.8 us; the launch traced here: 37.6 us
  Pallas kernels  35.7 us (94%)
  between operations  1.93 us (5%)
    pallas_call x1, Pallas kernels, shards(): pl.pallas_call(functools.partial(reduce_kernel, n_node, n_intra), out_sha...  34.9 us
    pallas_call x1, Pallas kernels, shards(): pl.pallas_call(store_kernel, out_shape=(out, out, out), in_specs=[vmem] *...  0.83 us

profile of v3, /device:TPU:0, one launch (start us, length us, event | category | flops | bytes accessed | tf_op | source)
XLA Modules:
  0.0 37.6 jit_solution(9683665424389188250)
XLA Ops:
  1.9 34.9 %shard_map.94 = (f32[384,128]{1,0:T(8,128)S(1)}, f32[384,128]{1,0:T(8,128)S(1)}, f32[384,128]{1,0:T(8,128)S(1)}) custom-call(bf16[3072,512]{1,0:T(8,128)(2,1)} %bitcast.1, s32[64,512]{1,0:T(8,128)} %sign_ref.1, f32[1]{0:T(128)S(6)} %copy.10.scale_ref, s32[1]{0:T(128)S(6)} %copy.11.step_ref, f32[384,128]{1,0:T(8,128)} %weight_ref.1, f32[384,128]{1,0:T(8,128)} %first_ref.1, ...), custom_call_target="tpu_custom_call" | custom-call | tf_op jit(solution)/shard_map/pallas_call | solution.py:723
  36.8 0.8 %shard_map.95 = (f32[384,128]{1,0:T(8,128)}, f32[384,128]{1,0:T(8,128)}, f32[384,128]{1,0:T(8,128)}) custom-call(f32[384,128]{1,0:T(8,128)S(1)} %get-tuple-element.6.refs_0_, f32[384,128]{1,0:T(8,128)S(1)} %get-tuple-element.7.refs_1_, f32[384,128]{1,0:T(8,128)S(1)} %get-tuple-element.8.refs_2_), custom_call_target="tpu_custom_call" | custom-call | tf_op jit(solution)/shard_map/pallas_call | solution.py:748

commit v4 on v3

--- a/solution.py
+++ b/solution.py
@@ -54,7 +54,7 @@
     owned = new_weight_ref.shape[0]
     z_rows, half = plan_rows(owned)
     zh = z_rows // 2
-    cut = (half // SUBS + 7) // 8 * 8
+    cut = (half * 4 // 9) // 8 * 8
     spans = ((0, cut), (cut, half - cut))
     raw_rows = half * 8 // 10 // 8 * 8
     raw_spans = ((0, raw_rows), (raw_rows, half - raw_rows))
@@ -114,8 +114,6 @@
         pl.semaphore_signal(barrier, inc=1, device_id=device, device_id_type=MESH)
     for q in range(CORES, min(SLOTS, n_intra)):
         load(q).start()
-    for copy in sides[1:]:
-        copy.start()
     table = parity_sign().astype(jnp.bfloat16)
     for a in range(2):
         for b in range(2):
@@ -278,6 +276,8 @@
     with scope("A_rotate"):
         most = lax.fori_loop(0, n_z, rotate, jnp.zeros((8, BLOCK), jnp.float32))
         peaks[me] = jnp.max(most, axis=0, keepdims=True)
+    for copy in sides[1:]:
+        copy.start()
     with scope("B_barrier"):
         pl.semaphore_wait(barrier, n_dev - 1)
 
@@ -520,10 +520,10 @@
 
         with scope("M2"):
             give_third(k - 1, 1)
+        with scope("M4"):
+            give_third(k, 0)
         with scope("Mz"):
             pl.when(k == last - 1)(z_finish)
-        with scope("M4"):
-            give_third(k, 0)
         return carry
 
     with scope("F0"):

time: 37.8 us -> 37.6 us (level)
  no operation moved by 1% of the time
where the time goes in v4:
time: 37.6 us; the launch traced here: 37.4 us
  Pallas kernels  35.5 us (94%)
  between operations  1.93 us (5%)
    pallas_call x1, Pallas kernels, shards(): pl.pallas_call(functools.partial(reduce_kernel, n_node, n_intra), out_sha...  34.6 us
    pallas_call x1, Pallas kernels, shards(): pl.pallas_call(store_kernel, out_shape=(out, out, out), in_specs=[vmem] *...  0.83 us

profile of v4, /device:TPU:0, one launch (start us, length us, event | category | flops | bytes accessed | tf_op | source)
XLA Modules:
  0.0 37.4 jit_solution(4262144294707807181)
XLA Ops:
  1.9 34.6 %shard_map.94 = (f32[384,128]{1,0:T(8,128)S(1)}, f32[384,128]{1,0:T(8,128)S(1)}, f32[384,128]{1,0:T(8,128)S(1)}) custom-call(bf16[3072,512]{1,0:T(8,128)(2,1)} %bitcast.1, s32[64,512]{1,0:T(8,128)} %sign_ref.1, f32[1]{0:T(128)S(6)} %copy.10.scale_ref, s32[1]{0:T(128)S(6)} %copy.11.step_ref, f32[384,128]{1,0:T(8,128)} %weight_ref.1, f32[384,128]{1,0:T(8,128)} %first_ref.1, ...), custom_call_target="tpu_custom_call" | custom-call | tf_op jit(solution)/shard_map/pallas_call | solution.py:723
  36.6 0.8 %shard_map.95 = (f32[384,128]{1,0:T(8,128)}, f32[384,128]{1,0:T(8,128)}, f32[384,128]{1,0:T(8,128)}) custom-call(f32[384,128]{1,0:T(8,128)S(1)} %get-tuple-element.6.refs_0_, f32[384,128]{1,0:T(8,128)S(1)} %get-tuple-element.7.refs_1_, f32[384,128]{1,0:T(8,128)S(1)} %get-tuple-element.8.refs_2_), custom_call_target="tpu_custom_call" | custom-call | tf_op jit(solution)/shard_map/pallas_call | solution.py:748

commit v5 on v4

--- a/solution.py
+++ b/solution.py
@@ -510,8 +510,7 @@
 
             @pl.when(k == 2)
             def _():
-                for s in range(SUBS):
-                    near_third(0, s, True)
+                near_third(0, 0, True)
 
             @pl.when(k > 2)
             def _():
@@ -520,6 +519,10 @@
 
         with scope("M2"):
             give_third(k - 1, 1)
+        @pl.when(k == 2)
+        def _():
+            near_third(0, 1, True)
+
         with scope("M4"):
             give_third(k, 0)
         with scope("Mz"):
@@ -536,10 +539,10 @@
             raw_piece()
         level_piece(1, 1)
     with scope("F1"):
+        first_sum(0, 1, True)
+        level_piece(2, 0)
         with scope("Fz"):
             z_inner(0, 1)
-        first_sum(0, 1, True)
-        level_piece(2, 0)
     begin()
     factor = (ones * top_value) / (ones * (127.0 * float(n_dev) * scale_ref[0]))
     column = pl.multiple_of(node * BLOCK, BLOCK)

time: 37.6 us -> 37.6 us (level)
  no operation moved by 1% of the time
where the time goes in v5:
time: 37.6 us; the launch traced here: 37.4 us
  Pallas kernels  35.5 us (94%)
  between operations  1.93 us (5%)
    pallas_call x1, Pallas kernels, shards(): pl.pallas_call(functools.partial(reduce_kernel, n_node, n_intra), out_sha...  34.6 us
    pallas_call x1, Pallas kernels, shards(): pl.pallas_call(store_kernel, out_shape=(out, out, out), in_specs=[vmem] *...  0.83 us

profile of v5, /device:TPU:0, one launch (start us, length us, event | category | flops | bytes accessed | tf_op | source)
XLA Modules:
  0.0 37.4 jit_solution(4361697334052380603)
XLA Ops:
  1.9 34.6 %shard_map.94 = (f32[384,128]{1,0:T(8,128)S(1)}, f32[384,128]{1,0:T(8,128)S(1)}, f32[384,128]{1,0:T(8,128)S(1)}) custom-call(bf16[3072,512]{1,0:T(8,128)(2,1)} %bitcast.1, s32[64,512]{1,0:T(8,128)} %sign_ref.1, f32[1]{0:T(128)S(6)} %copy.10.scale_ref, s32[1]{0:T(128)S(6)} %copy.11.step_ref, f32[384,128]{1,0:T(8,128)} %weight_ref.1, f32[384,128]{1,0:T(8,128)} %first_ref.1, ...), custom_call_target="tpu_custom_call" | custom-call | tf_op jit(solution)/shard_map/pallas_call | solution.py:726
  36.6 0.8 %shard_map.95 = (f32[384,128]{1,0:T(8,128)}, f32[384,128]{1,0:T(8,128)}, f32[384,128]{1,0:T(8,128)}) custom-call(f32[384,128]{1,0:T(8,128)S(1)} %get-tuple-element.6.refs_0_, f32[384,128]{1,0:T(8,128)S(1)} %get-tuple-element.7.refs_1_, f32[384,128]{1,0:T(8,128)S(1)} %get-tuple-element.8.refs_2_), custom_call_target="tpu_custom_call" | custom-call | tf_op jit(solution)/shard_map/pallas_call | solution.py:751

commit v6 on v4

--- a/solution.py
+++ b/solution.py
@@ -536,10 +536,10 @@
             raw_piece()
         level_piece(1, 1)
     with scope("F1"):
+        first_sum(0, 1, True)
+        level_piece(2, 0)
         with scope("Fz"):
             z_inner(0, 1)
-        first_sum(0, 1, True)
-        level_piece(2, 0)
     begin()
     factor = (ones * top_value) / (ones * (127.0 * float(n_dev) * scale_ref[0]))
     column = pl.multiple_of(node * BLOCK, BLOCK)
@@ -671,7 +671,12 @@
 
 def store_kernel(*refs):
     sems = refs[-1]
-    copies = [pltpu.make_async_copy(refs[n], refs[n + 3], sems.at[n]) for n in range(3)]
+    half = refs[0].shape[0] // 2
+    copies = [
+        pltpu.make_async_copy(refs[n].at[r], refs[n + 3].at[r], sems.at[n, h])
+        for h, r in enumerate((pl.ds(0, half), pl.ds(half, half)))
+        for n in range(3)
+    ]
     for copy in copies:
         copy.start()
     for copy in copies:
@@ -750,7 +755,7 @@
         out_shape=(out, out, out),
         in_specs=[vmem] * 3,
         out_specs=(anywhere,) * 3,
-        scratch_shapes=[dma((3,))],
+        scratch_shapes=[dma((3, 2))],
         compiler_params=pltpu.CompilerParams(vmem_limit_bytes=1 << 20),
     )(*outs)
 

time: 37.6 us -> 37.6 us (level)
  no operation moved by 1% of the time
where the time goes in v6:
time: 37.6 us; the launch traced here: 37.4 us
  Pallas kernels  35.5 us (94%)
  between operations  1.93 us (5%)
    pallas_call x1, Pallas kernels, shards(): pl.pallas_call(functools.partial(reduce_kernel, n_node, n_intra), out_sha...  34.6 us
    pallas_call x1, Pallas kernels, shards(): pl.pallas_call(store_kernel, out_shape=(out, out, out), in_specs=[vmem] *...  0.86 us

profile of v6, /device:TPU:0, one launch (start us, length us, event | category | flops | bytes accessed | tf_op | source)
XLA Modules:
  0.0 37.4 jit_solution(6199604072839781677)
XLA Ops:
  1.9 34.6 %shard_map.94 = (f32[384,128]{1,0:T(8,128)S(1)}, f32[384,128]{1,0:T(8,128)S(1)}, f32[384,128]{1,0:T(8,128)S(1)}) custom-call(bf16[3072,512]{1,0:T(8,128)(2,1)} %bitcast.1, s32[64,512]{1,0:T(8,128)} %sign_ref.1, f32[1]{0:T(128)S(6)} %copy.10.scale_ref, s32[1]{0:T(128)S(6)} %copy.11.step_ref, f32[384,128]{1,0:T(8,128)} %weight_ref.1, f32[384,128]{1,0:T(8,128)} %first_ref.1, ...), custom_call_target="tpu_custom_call" | custom-call | tf_op jit(solution)/shard_map/pallas_call | solution.py:728
  36.6 0.9 %shard_map.95 = (f32[384,128]{1,0:T(8,128)}, f32[384,128]{1,0:T(8,128)}, f32[384,128]{1,0:T(8,128)}) custom-call(f32[384,128]{1,0:T(8,128)S(1)} %get-tuple-element.6.refs_0_, f32[384,128]{1,0:T(8,128)S(1)} %get-tuple-element.7.refs_1_, f32[384,128]{1,0:T(8,128)S(1)} %get-tuple-element.8.refs_2_), custom_call_target="tpu_custom_call" | custom-call | tf_op jit(solution)/shard_map/pallas_call | solution.py:753
